TPU v7x, 32 devices: a whole 2x2x4 slice. The times are simulated.
32 devices in a mesh: job: 2 (over y), row: 4 (over z), col: 2 (over x), samp: 2 (over core).
Axes of the slice: x: 2, y: 2, z: 4, core: 2. Of those that a mesh axis runs over, the one named last changes fastest.
Arguments:
- pair_repr: bfloat16 [256, 128, 128], P(('job', 'row'), ('col', 'samp')), parts along dimension 0, may hold values from -100 to 100
- asym_id: int32 [256], P('job'), parts along dimension 0, may hold values from 0 to 7, never falling along the last dimension, each value on 1 to 32 neighbouring positions
- valid_len: int32 [2], P('job'), parts along dimension 0, may hold values from 64 to 128
- rel_embed: bfloat16 [128, 128], replicated, may hold values from -12 to 12
- pair_gain: float32 [128], replicated, may hold values from 0.25 to 1.75
- bias_weight: bfloat16 [128, 16], replicated, may hold values from -64 to 64
- tokens: bfloat16 [32, 128, 768], P(('job', 'col', 'samp'), 'row'), parts along dimension 0, may hold values from -6 to 6
- token_gain: float32 [1, 768], replicated, may hold values from 0.25 to 1.75
- qkv_weight: bfloat16 [1, 3, 768, 768], P(None, None, None, 'row'), may hold values from -0.21875 to 0.21875
- out_weight: bfloat16 [1, 768, 768], P(None, 'row'), may hold values from -0.21875 to 0.21875
Outputs:
- refined: bfloat16 [32, 128, 768], P(('job', 'col', 'samp'), 'row'), parts along dimension 0
There are 2 independent parts, one for each index of `job`. A program takes and returns all parts, laid end to end along the dimension named above; an argument that names none is the same for every part. Nothing has to cross between parts.
Inputs may be any that keep to these rules, and one draw needn't show every extreme that they name: `asym_id`: chain indices never fall along the tokens.
All inputs are finite; a program needn't handle non-finite values.
Results may differ from a plain program's by a relative error of at most 0.002.
The roundings to bfloat16 on the way count: a program that leaves them out, or rounds other values in their place, can miss the bound.
Values may be sent and summed in bfloat16 or wider, within the bound.
A program may use at most 64 MiB of HBM per device.

v0:
```python
import math

import jax
import jax.numpy as jnp
from jax import lax
from jax.sharding import PartitionSpec as P

HEAD_DIM = 48


epsilon = 1e-05


def normalize(values, gain_vector):
    average = jnp.mean(values, axis=-1, keepdims=True)
    centered = values - average
    variance = jnp.mean(centered * centered, axis=-1, keepdims=True)
    return centered * lax.rsqrt(variance + epsilon) * gain_vector


def bias_tile_of(pair_repr, asym_id, rel_embed, pair_gain, bias_weight):
    tile_rows, tile_cols, channels = pair_repr.shape
    bin_count = rel_embed.shape[0]
    reach_max = bin_count // 2 - 1
    first_row = lax.axis_index("row") * tile_rows
    first_col = lax.axis_index(("col", "samp")) * tile_cols
    row_ids = first_row + jnp.arange(tile_rows, dtype=jnp.int32)
    col_ids = first_col + jnp.arange(tile_cols, dtype=jnp.int32)
    row_chain = lax.dynamic_slice_in_dim(asym_id, first_row, tile_rows, 0)
    col_chain = lax.dynamic_slice_in_dim(asym_id, first_col, tile_cols, 0)
    offset = jnp.clip(row_ids[:, None] - col_ids[None, :], -reach_max, reach_max) + reach_max
    bin_ids = jnp.where(row_chain[:, None] == col_chain[None, :], offset, bin_count - 1)
    onehot = (
        bin_ids.reshape(-1)[:, None] == jnp.arange(bin_count, dtype=jnp.int32)[None, :]
    ).astype(jnp.bfloat16)
    summed = pair_repr.reshape(-1, channels).astype(jnp.float32) + jnp.dot(
        onehot, rel_embed, preferred_element_type=jnp.float32
    )
    normed = normalize(summed, pair_gain).astype(jnp.bfloat16)
    projected = lax.dot_general(
        bias_weight, normed, (((0,), (1,)), ((), ())), preferred_element_type=jnp.float32
    )
    return projected.reshape(bias_weight.shape[1], tile_rows, tile_cols)


def attend(queries, key_rows, value_rows, pair_bias, keymask, score_scale):
    head_count, query_count, key_count = pair_bias.shape
    model_width = queries.shape[-1]
    head_width = model_width // head_count
    query_h = queries.reshape(query_count, head_count, head_width)
    key_h = key_rows.reshape(key_count, head_count, head_width)
    value_h = value_rows.reshape(key_count, head_count, head_width)
    scores = (
        jnp.einsum("ihd,jhd->hij", query_h, key_h, preferred_element_type=jnp.float32) * score_scale
        + pair_bias
    )
    scores = jnp.where(keymask[None, None, :], scores, -1e30)
    row_max = jnp.max(scores, axis=-1, keepdims=True)
    weights = jnp.where(keymask[None, None, :], jnp.exp(scores - row_max), 0.0)
    row_total = jnp.sum(weights, axis=-1, keepdims=True)
    probs = (weights / row_total).astype(jnp.bfloat16)
    attended = jnp.einsum("hij,jhd->ihd", probs, value_h, preferred_element_type=jnp.float32)
    return attended.reshape(query_count, model_width).astype(jnp.bfloat16)


def per_device(
    pair_repr,
    asym_id,
    valid_len,
    rel_embed,
    pair_gain,
    bias_weight,
    tokens,
    token_gain,
    qkv_weight,
    out_weight,
):
    sample_count, token_rows, model_width = tokens.shape
    total_tokens = asym_id.shape[0]
    keymask = jnp.arange(total_tokens, dtype=jnp.int32) < valid_len[0]
    score_scale = 1.0 / math.sqrt(HEAD_DIM)
    bias_tile = bias_tile_of(pair_repr, asym_id, rel_embed, pair_gain, bias_weight)
    head_tile = lax.all_to_all(bias_tile, "row", split_axis=0, concat_axis=1, tiled=True)
    pair_bias = lax.all_gather(head_tile, ("col", "samp"), axis=2, tiled=True)

    def one_sample(sample_item):
        return attend(
            sample_item[0], sample_item[1], sample_item[2], pair_bias, keymask, score_scale
        )

    current = tokens
    normed = normalize(current.astype(jnp.float32), token_gain[0]).astype(jnp.bfloat16)
    layer_weight = qkv_weight[0]
    projected = jnp.einsum(
        "snc,pcw->psnw",
        lax.all_gather(normed, "row", axis=1, tiled=True),
        layer_weight,
        preferred_element_type=jnp.float32,
    ).astype(jnp.bfloat16)
    head_out = lax.map(one_sample, (projected[0], projected[1], projected[2]))
    attended = lax.all_to_all(head_out, "row", split_axis=1, concat_axis=2, tiled=True)
    flattened = attended.reshape(sample_count * token_rows, model_width)
    update = jnp.dot(
        flattened,
        lax.all_gather(out_weight[0], "row", axis=0, tiled=True),
        preferred_element_type=jnp.float32,
    )
    current = (
        current.astype(jnp.float32) + update.reshape(sample_count, token_rows, model_width)
    ).astype(jnp.bfloat16)
    return current


def solution(mesh):
    return jax.shard_map(
        per_device,
        mesh=mesh,
        in_specs=(
            P(("job", "row"), ("col", "samp"), None),
            P("job"),
            P("job"),
            P(),
            P(),
            P(),
            P(("job", "col", "samp"), "row", None),
            P(),
            P(None, None, None, "row"),
            P(None, "row", None),
        ),
        out_specs=P(("job", "col", "samp"), "row", None),
        check_vma=False,
    )
```

profile of v0, /device:TPU:0, one launch (start us, length us, event | category | flops | bytes accessed | tf_op | source)
XLA Modules:
  0.0 80.8 jit_solution(11071996184877069261)
XLA Ops:
  6.5 0.0 copy-start
  6.5 0.0 copy-start.2
  6.5 0.8 %fusion.27 = (s32[32]{0:T(128)S(1)}, s32[32]{0:T(128)S(1)}) fusion(s32[128]{0:T(128)} %param.13, s32[]{:T(128)S(6)} %select_n.24, s32[]{:T(128)S(6)} %select_n.25), kind=kLoop, calls=%fused_computation.52 | loop fusion | bytes 520 | tf_op jit(solution)/shard_map/dynamic_slice | solution.py:29
  7.4 0.1 add_select_fusion
  7.5 0.1 select_n.27
  7.5 1.0 %bitcast_convert_fusion = f32[1024,128]{1,0:T(8,128)S(1)} fusion(bf16[32,32,128]{2,1,0:T(8,128)(2,1)} %param.12), kind=kLoop, calls=%fused_computation.36 | loop fusion | flops 131072 | bytes 786432 | tf_op jit(solution)/shard_map/convert_element_type | solution.py:36
  8.5 0.0 copy-start.3
  8.5 0.0 copy-start.5
  8.5 0.2 copy.21
  8.7 0.0 copy-done.2
  8.8 1.0 %fusion.28 = (f32[1024]{0:T(1024)S(1)}, f32[1024,128]{0,1:T(8,128)S(1)}) fusion(f32[1024,128]{0,1:T(8,128)S(1)} %copy.21, bf16[128,128]{1,0:T(8,128)(2,1)S(1)} %copy-done.2, s32[1024]{0:T(1024)S(1)} %select_n.27), kind=kOutput, calls=%fused_computation.53 | convolution fusion | flops 33946624 | bytes 1089536 | tf_op jit(solution)/shard_map/dot_general | solution.py:36
  9.7 0.0 copy-start.1
  9.7 0.1 multiply_reduce_fusion
  9.8 0.0 copy-start.4
  9.8 0.0 copy-done.3
  9.9 0.0 copy-done.5
  9.9 0.2 convolution_bitcast_fusion
  10.1 0.1 reshape.112
  10.2 0.8 reshape.122
  11.0 6.3 %all-to-all-start = ((f32[4,1,4096]{2,1,0:T(1,128)}), f32[4,1,4096]{2,1,0:T(1,128)S(1)}, u32[]{:S(2)}, u32[]{:S(2)}) async-start(f32[4,1,4096]{2,1,0:T(1,128)} %reshape.122), calls=%async_computation | async-start | bytes 131072 | tf_op jit(solution)/shard_map/all_to_all | solution.py:83
  17.3 0.0 all-gather.3.cloned.1.call-start
  17.4 0.7 all-gather.3.cloned.1.call-update
  18.1 0.0 copy-done.1
  18.1 0.1 convert_reduce_fusion
  18.2 0.2 fusion.19
  18.4 0.0 copy-done.4
  18.4 0.1 fusion.21
  18.6 24.0 %all_gather.9 = bf16[4,128,768]{2,1,0:T(8,128)(2,1)S(1)} all-gather(bf16[4,32,768]{2,1,0:T(8,128)(2,1)S(1)} %fusion.21), channel_id=1, replica_groups=mesh['job'=2,'row'=4,'col'=2,'samp'=2] {'row'}, dimensions={1}, use_global_device_ids=true | all-gather | bytes 983040 | tf_op jit(solution)/shard_map/all_gather | solution.py:96
  42.6 0.0 copy-done
  42.6 0.6 fusion.10
  43.3 0.0 all-to-all-done
  43.3 0.5 broadcast.98
  43.8 0.8 %reduce.1 = f32[4,4096]{1,0:T(4,128)S(1)} reduce(f32[4,1,4096]{2,1,0:T(1,128)S(1)} %all-to-all-done, f32[]{:T(128)} %broadcast.98), dimensions={1}, to_apply=%all_to_all.24.reduce_sub_computation | reduce | bytes 131076 | tf_op jit(solution)/shard_map/all_to_all | solution.py:83
  44.7 0.1 reshape.123
  44.8 0.1 copy.22
  44.9 0.2 all_to_all.27
  45.1 5.8 %all_gather.10 = f32[4,128,128]{1,2,0:T(8,128)S(1)} all-gather(f32[4,128,32]{1,2,0:T(8,128)S(1)} %all_to_all.27), channel_id=1, replica_groups=mesh['job'=2,'row'=4,'col'=2,'samp'=2] {'col','samp'}, dimensions={2}, use_global_device_ids=true | all-gather | bytes 327680 | tf_op jit(solution)/shard_map/all_gather | solution.py:84
  50.9 5.3 %while.11 = (s32[]{:T(128)}, bf16[4,128,192]{1,2,0:T(8,128)(2,1)S(1)}, bf16[4,128,192]{1,2,0:T(8,128)(2,1)S(1)}, bf16[4,128,192]{1,2,0:T(8,128)(2,1)S(1)}, bf16[...) while((s32[]{:T(128)}, ...), condition=%wide.region_7.8_spmd.clone, body=%wide.region_4.7_spmd.clone.sunk | while | flops 13263744 | bytes 1643109 | solution.py:100
  50.9 0.6 iota_compare_fusion.4
  51.5 0.2 fusion.49
  51.8 0.1 fusion.50
  51.9 0.2 convolution_convert_fusion.3
  52.2 0.7 iota_compare_fusion.4
  52.9 0.2 fusion.49
  53.1 0.1 fusion.50
  53.3 0.2 convolution_convert_fusion.3
  53.6 0.7 iota_compare_fusion.4
  54.2 0.2 fusion.49
  54.5 0.1 fusion.50
  54.6 0.2 convolution_convert_fusion.3
  54.9 0.7 iota_compare_fusion.4
  55.6 0.2 fusion.49
  55.8 0.1 fusion.50
  55.9 0.2 convolution_convert_fusion.3
  56.2 0.2 copy.23
  56.4 14.7 %all_to_all.33 = bf16[4,128,192]{2,0,1:T(4,128)(2,1)S(1)} all-to-all(bf16[4,128,192]{2,0,1:T(4,128)(2,1)S(1)} %copy.23), channel_id=1, replica_groups=mesh['job'=2,'row'=4,'col'=2,'samp'=2] {'row'}, dimensions={1} | all-to-all | bytes 393216 | tf_op jit(solution)/shard_map/all_to_all | solution.py:101
  71.2 0.2 copy.25
  71.4 0.2 dot_general.26
  71.6 0.0 all-gather.3.cloned.1.call-done
  71.7 2.3 %fusion.12 = bf16[4,32,768]{2,1,0:T(8,128)(2,1)} fusion(bf16[4,32,768]{2,1,0:T(8,128)(2,1)S(1)} %dot_general.26, bf16[1,768,768]{2,1,0:T(8,128)(2,1)} %all-gather.3.cloned.1.call-done, bf16[4,32,768]{2,1,0:T(8,128)(2,1)S(1)} %copy-done.1), kind=kOutput, calls=%fused_computation.22 | convolution fusion | flops 151289856 | bytes 1769472 | tf_op jit(solution)/shard_map/dot_general | solution.py:103
  (21 shorter events, 0.3 us)
Async XLA Ops:
  6.5 36.1 %copy-start = (bf16[1,3,768,192]{2,3,1,0:T(8,128)(2,1)S(1)}, bf16[1,3,768,192]{2,3,1,0:T(8,128)(2,1)}, u32[]{:S(2)}) copy-start(bf16[1,3,768,192]{2,3,1,0:T(8,128)(2,1)} %param.20) | copy-start | bytes 2654212
  6.5 2.2 %copy-start.2 = (bf16[128,128]{1,0:T(8,128)(2,1)S(1)}, bf16[128,128]{1,0:T(8,128)(2,1)}, u32[]{:S(2)}) copy-start(bf16[128,128]{1,0:T(8,128)(2,1)} %param.15) | copy-start | bytes 98308
  8.5 1.3 %copy-start.3 = (bf16[128,16]{0,1:T(8,128)(2,1)S(1)}, bf16[128,16]{0,1:T(8,128)(2,1)}, u32[]{:S(2)}) copy-start(bf16[128,16]{0,1:T(8,128)(2,1)} %param.17) | copy-start | bytes 12292
  8.5 1.3 %copy-start.5 = (f32[128]{0:T(128)S(1)}, f32[128]{0:T(128)}, u32[]{:S(2)}) copy-start(f32[128]{0:T(128)} %param.16) | copy-start | bytes 1540
  9.7 8.4 %copy-start.1 = (bf16[4,32,768]{2,1,0:T(8,128)(2,1)S(1)}, bf16[4,32,768]{2,1,0:T(8,128)(2,1)}, u32[]{:S(2)}) copy-start(bf16[4,32,768]{2,1,0:T(8,128)(2,1)} %param.18) | copy-start | bytes 589828
  9.8 8.6 %copy-start.4 = (f32[1,768]{1,0:T(1,128)S(1)}, f32[1,768]{1,0:T(1,128)}, u32[]{:S(2)}) copy-start(f32[1,768]{1,0:T(1,128)} %param.19) | copy-start | bytes 9220
  11.0 32.3 %all-to-all-start = ((f32[4,1,4096]{2,1,0:T(1,128)}), f32[4,1,4096]{2,1,0:T(1,128)S(1)}, u32[]{:S(2)}, u32[]{:S(2)}) async-start(f32[4,1,4096]{2,1,0:T(1,128)} %reshape.122), calls=%async_computation | async-start | bytes 131072 | tf_op jit(solution)/shard_map/all_to_all | solution.py:83
  17.3 54.3 %all-gather.3.cloned.1.call-start = ((), (), s32[]{:S(2)}) async-start(), calls=%async_computation.2 | async-start | bytes 1474560 | tf_op jit(solution)/shard_map/all_gather | solution.py:105
Sparse Core Ops, SparseCore 0:
  19.7 35.6 all-gather.2
where the time goes:
time: 81.1 us; the launch traced here: 80.8 us
  blocking collectives  44.5 us (55%)
  between operations  13.6 us (17%)
  starting transfers between devices  6.35 us (8%)
  matrix products  6.03 us (7%)
  other arithmetic  5.46 us (7%)
  local copies, waits for them, and re-layouts  3.84 us (5%)
    all_gather x1, blocking collectives, per_device(): lax.all_gather(normed, 'row', axis=1, tiled=True)  24 us
    all_to_all x1, blocking collectives, per_device(): lax.all_to_all(head_out, 'row', split_axis=1, concat_axis=2, tiled=True)  14.7 us
    all_to_all x1, starting transfers between devices, per_device(): lax.all_to_all(bias_tile, 'row', split_axis=0, concat_axis=1, tiled=True)  6.35 us
    all_gather x1, blocking collectives, per_device(): pair_bias = lax.all_gather(head_tile, ('col', 'samp'), axis=2, tiled=True)  5.78 us
    lt x4, other arithmetic, per_device(): keymask = jnp.arange(total_tokens, dtype=jnp.int32) < valid_len[0]  2.61 us
    dot_general x1, matrix products, per_device(): jnp.dot(flattened, lax.all_gather(out_weight[0], 'row', axis=0, tiled=Tru...  2.28 us
  transfers between devices with their start and end apart: 2, of which 0 were waited for; matrix products, arithmetic and copies ran while one was open for 11% of the time, Pallas kernels for 0%

commit v1 on v0

v1 whole, which is shorter than its diff:
```python
import functools
import math

import jax
import jax.numpy as jnp
from jax import lax
from jax.experimental import pallas as pl
from jax.experimental.pallas import tpu as pltpu
from jax.sharding import PartitionSpec as P

HEAD_DIM = 48
EPSILON = 1e-05
LANES = 128
MESH = pl.DeviceIdType.MESH


def normalize(values, gain_vector):
    average = jnp.mean(values, axis=-1, keepdims=True)
    centered = values - average
    variance = jnp.mean(centered * centered, axis=-1, keepdims=True)
    return centered * lax.rsqrt(variance + EPSILON) * gain_vector


def kernel(
    axes,
    asym,
    valid,
    pair_hbm,
    rel_hbm,
    pair_gain_hbm,
    bias_weight_hbm,
    tokens_hbm,
    token_gain_hbm,
    qkv_hbm,
    out_weight_hbm,
    out,
    pair,
    rel,
    pair_gain,
    bias_weight,
    token_gain,
    qkv,
    tok,
    ow,
    bias_send,
    bias_recv,
    bias,
    query,
    key,
    value,
    attended,
    heads_in,
    local_sem,
    tok_local,
    tok_send,
    tok_recv,
    bz_send,
    bz_recv,
    bp_send,
    bp_recv,
    own_bias_sem,
    oz_send,
    oz_recv,
    op_send,
    op_recv,
    at_send,
    at_recv,
):
    n_job, n_row, n_col, n_samp = axes
    job, me = lax.axis_index("job"), lax.axis_index("row")
    col, samp = lax.axis_index("col"), lax.axis_index("samp")
    samples, token_rows, width = tokens_hbm.shape
    total = n_row * token_rows
    tile_rows, tile_cols, channels = pair.shape
    bins = rel.shape[0]
    n_plane = n_col * n_samp
    plane = col * n_samp + samp
    all_heads = bias_weight.shape[1]
    local_heads = all_heads // n_row
    head_rows = bias_recv.shape[2]
    fold = LANES // tile_cols
    stripes = tile_rows // fold
    out_rows = ow.shape[1]
    pieces = oz_recv.shape[0] // n_row
    piece_rows = out_rows // pieces
    shared = pieces > 1
    group = job * n_samp + samp if shared else 0
    local_width = local_heads * HEAD_DIM

    def row_peer(k):
        return lax.rem(me + k, n_row)

    def plane_peer(k):
        other = lax.rem(plane + k, n_plane)
        return {"col": lax.div(other, n_samp), "samp": lax.rem(other, n_samp)}, other

    def group_peer(k):
        other = lax.rem(group + k, pieces)
        return {"job": lax.div(other, n_samp), "samp": lax.rem(other, n_samp)}, other

    loads = {}
    for index, (name, source, target) in enumerate(
        (
            ("pair", pair_hbm, pair),
            ("rel", rel_hbm, rel),
            ("pair_gain", pair_gain_hbm, pair_gain),
            ("bias_weight", bias_weight_hbm, bias_weight),
            ("token_gain", token_gain_hbm, token_gain),
            ("qkv", qkv_hbm.at[0], qkv),
            ("ow", out_weight_hbm.at[0], ow.at[me]),
        )
    ):
        loads[name] = pltpu.make_async_copy(source, target, local_sem.at[index])
    tok_loads = [
        pltpu.make_async_copy(tokens_hbm.at[s], tok.at[s, me], tok_local.at[s]) for s in range(samples)
    ]
    tok_loads[0].start()
    for name in ("pair", "rel", "pair_gain", "bias_weight"):
        loads[name].start()
    for s in range(1, samples):
        tok_loads[s].start()
    for name in ("token_gain", "qkv", "ow"):
        loads[name].start()

    barrier = pltpu.get_barrier_semaphore()
    for k in range(1, n_row):
        pl.semaphore_signal(barrier, inc=1, device_id={"row": row_peer(k)}, device_id_type=MESH)
    for k in range(1, n_plane):
        pl.semaphore_signal(barrier, inc=1, device_id=plane_peer(k)[0], device_id_type=MESH)
    if shared:
        for k in range(1, pieces):
            pl.semaphore_signal(barrier, inc=1, device_id=group_peer(k)[0], device_id_type=MESH)
    pl.semaphore_wait(barrier, (n_row - 1) + (n_plane - 1) + ((pieces - 1) if shared else 0))

    has_right, has_left = me < n_row - 1, me > 0
    right, left = jnp.minimum(me + 1, n_row - 1), jnp.maximum(me - 1, 0)

    def tok_copy(s, source, direction):
        return pltpu.make_async_remote_copy(
            src_ref=tok.at[s, source],
            dst_ref=tok.at[s, source],
            send_sem=tok_send.at[direction, s, source],
            recv_sem=tok_recv.at[s, source],
            device_id={"row": left if direction else right},
            device_id_type=MESH,
        )

    def send_own(s):
        tok_loads[s].wait()

        @pl.when(has_right)
        def _():
            tok_copy(s, me, 0).start()

        @pl.when(has_left)
        def _():
            tok_copy(s, me, 1).start()

    def pass_on(s):
        for k in range(1, n_row):

            @pl.when(me - k >= 0)
            def _():
                source = jnp.maximum(me - k, 0)
                tok_copy(s, source, 0).wait_recv()

                @pl.when(has_right)
                def _():
                    tok_copy(s, source, 0).start()

            @pl.when(me + k < n_row)
            def _():
                source = jnp.minimum(me + k, n_row - 1)
                tok_copy(s, source, 1).wait_recv()

                @pl.when(has_left)
                def _():
                    tok_copy(s, source, 1).start()

    def finish_tok_sends(s):
        for k in range(0, n_row):

            @pl.when(jnp.logical_and(me - k >= 0, has_right))
            def _():
                tok_copy(s, jnp.maximum(me - k, 0), 0).wait_send()

            @pl.when(jnp.logical_and(me + k < n_row, has_left))
            def _():
                tok_copy(s, jnp.minimum(me + k, n_row - 1), 1).wait_send()

    for s in range(min(2, samples)):
        send_own(s)

    for name in ("pair", "rel", "pair_gain", "bias_weight"):
        loads[name].wait()
    first_row, first_col = me * tile_rows, plane * tile_cols
    sub = lax.broadcasted_iota(jnp.int32, (tile_cols, LANES), 0)
    lane = lax.broadcasted_iota(jnp.int32, (tile_cols, LANES), 1)
    col_chain = jnp.zeros((tile_cols, LANES), jnp.int32)
    for j in range(tile_cols):
        col_chain = jnp.where(sub == j, asym[first_col + j], col_chain)
    reach = bins // 2 - 1
    turned_weight = bias_weight[...].astype(jnp.float32).T.astype(jnp.bfloat16)
    for t in range(stripes):
        hots, rows = [], []
        for q in range(fold):
            i = q * stripes + t
            offset = jnp.clip(first_row + i - first_col - sub, -reach, reach) + reach
            bin_ids = jnp.where(col_chain == asym[first_row + i], offset, bins - 1)
            hots.append(jnp.where(bin_ids == lane, 1.0, 0.0).astype(jnp.bfloat16))
            rows.append(pair[i].astype(jnp.float32))
        summed = jnp.concatenate(rows, axis=0) + jnp.dot(
            jnp.concatenate(hots, axis=0), rel[...], preferred_element_type=jnp.float32
        )
        normed = normalize(summed, pair_gain[...]).astype(jnp.bfloat16)
        projected = lax.dot_general(
            turned_weight, normed, (((1,), (1,)), ((), ())), preferred_element_type=jnp.float32
        )
        bias_send[pl.ds(t, all_heads, stride=stripes), :] = projected

    def bias_part(dest):
        return bias_send.at[pl.ds(pl.multiple_of(dest * head_rows, head_rows), head_rows)]

    def bias_row_copy(k):
        dest = row_peer(k)
        return pltpu.make_async_remote_copy(
            src_ref=bias_part(dest),
            dst_ref=bias_recv.at[me, plane],
            send_sem=bz_send.at[k],
            recv_sem=bz_recv.at[k],
            device_id={"row": dest},
            device_id_type=MESH,
        )

    def bias_plane_copy(k, m):
        device, _ = plane_peer(m)
        source = row_peer(n_row - k)
        return pltpu.make_async_remote_copy(
            src_ref=bias_part(me) if k == 0 else bias_recv.at[source, plane],
            dst_ref=bias_recv.at[source, plane],
            send_sem=bp_send.at[k, m],
            recv_sem=bp_recv.at[k, m],
            device_id=device,
            device_id_type=MESH,
        )

    def bias_plane_wait(k, m):
        source = row_peer(n_row - k)
        origin = lax.rem(plane + n_plane - m, n_plane)
        pltpu.make_async_remote_copy(
            src_ref=bias_recv.at[source, origin],
            dst_ref=bias_recv.at[source, origin],
            send_sem=bp_send.at[k, m],
            recv_sem=bp_recv.at[k, m],
            device_id=plane_peer(m)[0],
            device_id_type=MESH,
        ).wait_recv()

    def bias_row_wait(k):
        source = row_peer(n_row - k)
        pltpu.make_async_remote_copy(
            src_ref=bias_recv.at[source, plane],
            dst_ref=bias_recv.at[source, plane],
            send_sem=bz_send.at[k],
            recv_sem=bz_recv.at[k],
            device_id={"row": row_peer(k)},
            device_id_type=MESH,
        ).wait_recv()

    for k in range(1, n_row):
        bias_row_copy(k).start()
    own_bias = pltpu.make_async_copy(bias_part(me), bias_recv.at[me, plane], own_bias_sem)
    own_bias.start()
    for m in range(1, n_plane):
        bias_plane_copy(0, m).start()

    def ow_part(source, piece):
        if not shared:
            return ow.at[source]
        return ow.at[source, pl.ds(pl.multiple_of(piece * piece_rows, piece_rows), piece_rows)]

    def ow_row_copy(k):
        return pltpu.make_async_remote_copy(
            src_ref=ow_part(me, group),
            dst_ref=ow_part(me, group),
            send_sem=oz_send.at[k],
            recv_sem=oz_recv.at[k],
            device_id={"row": row_peer(k)},
            device_id_type=MESH,
        )

    def ow_row_wait(k):
        source = row_peer(n_row - k)
        pltpu.make_async_remote_copy(
            src_ref=ow_part(source, group),
            dst_ref=ow_part(source, group),
            send_sem=oz_send.at[k],
            recv_sem=oz_recv.at[k],
            device_id={"row": row_peer(k)},
            device_id_type=MESH,
        ).wait_recv()

    def ow_group_copy(k, m):
        source = row_peer(n_row - k)
        return pltpu.make_async_remote_copy(
            src_ref=ow_part(source, group),
            dst_ref=ow_part(source, group),
            send_sem=op_send.at[k, m],
            recv_sem=op_recv.at[k, m],
            device_id=group_peer(m)[0],
            device_id_type=MESH,
        )

    def ow_group_wait(k, m):
        source = row_peer(n_row - k)
        origin = lax.rem(group + pieces - m, pieces)
        pltpu.make_async_remote_copy(
            src_ref=ow_part(source, origin),
            dst_ref=ow_part(source, origin),
            send_sem=op_send.at[k, m],
            recv_sem=op_recv.at[k, m],
            device_id=group_peer(m)[0],
            device_id_type=MESH,
        ).wait_recv()

    head_of_lane = lax.broadcasted_iota(jnp.int32, (total, local_width), 1)
    head_masks = [
        jnp.logical_and(head_of_lane >= h * HEAD_DIM, head_of_lane < (h + 1) * HEAD_DIM)
        for h in range(local_heads)
    ]
    scale = 1.0 / math.sqrt(HEAD_DIM)

    def project(s):
        rows = tok[s].reshape(total, width).astype(jnp.float32)
        normed = normalize(rows, token_gain[...]).astype(jnp.bfloat16)
        query[s] = jnp.dot(normed, qkv[0], preferred_element_type=jnp.float32).astype(jnp.bfloat16)
        key[s] = jnp.dot(normed, qkv[1], preferred_element_type=jnp.float32).astype(jnp.bfloat16)
        value[s] = jnp.dot(normed, qkv[2], preferred_element_type=jnp.float32).astype(jnp.bfloat16)

    def attend(s):
        keys, values = key[s].astype(jnp.float32), value[s].astype(jnp.float32)
        keys = jnp.concatenate(
            [jnp.where(mask, keys, 0.0).astype(jnp.bfloat16) for mask in head_masks], axis=0
        )
        values = jnp.concatenate(
            [jnp.where(mask, values, 0.0).astype(jnp.bfloat16) for mask in head_masks], axis=0
        )
        scores = lax.dot_general(
            query[s], keys, (((1,), (1,)), ((), ())), preferred_element_type=jnp.float32
        )
        probs = []
        for h in range(local_heads):
            mine = scores[:, h * total : (h + 1) * total] * scale + bias[:, h * total : (h + 1) * total]
            weights = jnp.exp(mine - jnp.max(mine, axis=-1, keepdims=True))
            inverse = 1.0 / jnp.sum(weights, axis=-1, keepdims=True)
            probs.append((weights * inverse).astype(jnp.bfloat16))
        mixed = jnp.dot(
            jnp.concatenate(probs, axis=1), values, preferred_element_type=jnp.float32
        ).astype(jnp.bfloat16)
        attended[s] = mixed.reshape(n_row, token_rows, local_width)

    def att_copy(s, k):
        dest = row_peer(k)
        return pltpu.make_async_remote_copy(
            src_ref=attended.at[s, dest],
            dst_ref=heads_in.at[me, s],
            send_sem=at_send.at[s, k],
            recv_sem=at_recv.at[s, k],
            device_id={"row": dest},
            device_id_type=MESH,
        )

    def att_wait(s, k):
        source = row_peer(n_row - k)
        pltpu.make_async_remote_copy(
            src_ref=heads_in.at[source, s],
            dst_ref=heads_in.at[source, s],
            send_sem=at_send.at[s, k],
            recv_sem=at_recv.at[s, k],
            device_id={"row": row_peer(k)},
            device_id_type=MESH,
        ).wait_recv()

    def give(s):
        for k in range(1, n_row):
            att_copy(s, k).start()
        heads_in[me, s] = attended[s, me]

    pass_on(0)
    for s in range(2, min(3, samples)):
        send_own(s)
    for k in range(1, n_row):
        bias_row_wait(k)
        for m in range(1, n_plane):
            bias_plane_copy(k, m).start()
    for name in ("token_gain", "qkv"):
        loads[name].wait()
    project(0)
    for s in range(1, samples):
        pass_on(s)
        if s + 2 < samples:
            send_own(s + 2)
        if s == 1:
            loads["ow"].wait()
            for k in range(1, n_row):
                ow_row_copy(k).start()
        project(s)
        if s == 1:
            own_bias.wait()
            for k in range(n_row):
                for m in range(1, n_plane):
                    bias_plane_wait(k, m)
            lanes_at = lax.broadcasted_iota(jnp.int32, (head_rows, LANES), 1)
            for tile in range(total // LANES):
                padded = lanes_at[:stripes] + tile * LANES >= valid[0]
                for r in range(n_row):
                    parts = [bias_recv[r, tile * fold + m] for m in range(fold)]
                    for q in range(fold):
                        whole = None
                        for m in range(fold):
                            shift = ((m - q) % fold) * tile_cols
                            turned = pltpu.roll(parts[m], shift, 1) if shift else parts[m]
                            whole = (
                                turned
                                if whole is None
                                else jnp.where(lanes_at >= m * tile_cols, turned, whole)
                            )
                        at = r * tile_rows + q * stripes
                        for h in range(local_heads):
                            bias[
                                at : at + stripes,
                                h * total + tile * LANES : h * total + (tile + 1) * LANES,
                            ] = jnp.where(padded, -1e30, whole[h * stripes : (h + 1) * stripes])
        if s == 2 and shared:
            for k in range(1, n_row):
                ow_row_wait(k)
                for m in range(1, pieces):
                    ow_group_copy(k, m).start()
        attend(s - 1)
        give(s - 1)
    attend(samples - 1)
    give(samples - 1)

    for k in range(1, n_row):
        if shared:
            for m in range(1, pieces):
                ow_group_wait(k, m)
        else:
            ow_row_wait(k)

    def update_of(source):
        flat = heads_in[source].reshape(samples * token_rows, local_width)
        return jnp.dot(flat, ow[source], preferred_element_type=jnp.float32)

    update = tok[:, me].reshape(samples * token_rows, width).astype(jnp.float32) + 0.0
    product = update_of(me)
    for k in range(1, n_row):
        for s in range(samples):
            att_wait(s, k)
        product = product + update_of(row_peer(n_row - k))
    out[...] = (update + product).astype(out.dtype).reshape(samples, token_rows, width)

    for s in range(samples):
        finish_tok_sends(s)
        for k in range(1, n_row):
            att_copy(s, k).wait_send()
    for k in range(1, n_row):
        bias_row_copy(k).wait_send()
        ow_row_copy(k).wait_send()
        if shared:
            for m in range(1, pieces):
                ow_group_copy(k, m).wait_send()
    for k in range(n_row):
        for m in range(1, n_plane):
            bias_plane_copy(k, m).wait_send()


def per_device(
    axes,
    pair_repr,
    asym_id,
    valid_len,
    rel_embed,
    pair_gain,
    bias_weight,
    tokens,
    token_gain,
    qkv_weight,
    out_weight,
):
    n_job, n_row, n_col, n_samp = axes
    samples, token_rows, width = tokens.shape
    total = n_row * token_rows
    n_plane = n_col * n_samp
    heads = bias_weight.shape[1]
    local_heads = heads // n_row
    tile_rows, tile_cols, channels = pair_repr.shape
    local_width = qkv_weight.shape[-1]
    out_rows = out_weight.shape[1]
    pieces = n_job * n_samp
    if out_rows % (16 * pieces) or pieces == 1:
        pieces = 1
    stripes = tile_rows // (LANES // tile_cols)
    head_rows = local_heads * stripes
    bf16, f32 = jnp.bfloat16, jnp.float32
    dma = pltpu.SemaphoreType.DMA
    any_spec = pl.BlockSpec(memory_space=pl.ANY)
    smem_spec = pl.BlockSpec(memory_space=pltpu.SMEM)
    return pl.pallas_call(
        functools.partial(kernel, axes),
        out_shape=jax.ShapeDtypeStruct(tokens.shape, tokens.dtype),
        in_specs=[smem_spec] * 2 + [any_spec] * 8,
        out_specs=pl.BlockSpec(memory_space=pltpu.VMEM),
        scratch_shapes=[
            pltpu.VMEM(pair_repr.shape, bf16),
            pltpu.VMEM(rel_embed.shape, bf16),
            pltpu.VMEM((1, channels), f32),
            pltpu.VMEM(bias_weight.shape, bf16),
            pltpu.VMEM(token_gain.shape, f32),
            pltpu.VMEM(qkv_weight.shape[1:], bf16),
            pltpu.VMEM((samples, n_row, token_rows, width), bf16),
            pltpu.VMEM((n_row, out_rows, width), bf16),
            pltpu.VMEM((heads * stripes, LANES), f32),
            pltpu.VMEM((n_row, n_plane, head_rows, LANES), f32),
            pltpu.VMEM((total, local_heads * total), f32),
            pltpu.VMEM((samples, total, local_width), bf16),
            pltpu.VMEM((samples, total, local_width), bf16),
            pltpu.VMEM((samples, total, local_width), bf16),
            pltpu.VMEM((samples, n_row, token_rows, local_width), bf16),
            pltpu.VMEM((n_row, samples, token_rows, local_width), bf16),
            dma((7,)),
            dma((samples,)),
            dma((2, samples, n_row)),
            dma((samples, n_row)),
            dma((n_row,)),
            dma((n_row,)),
            dma((n_row, n_plane)),
            dma((n_row, n_plane)),
            dma,
            dma((n_row,)),
            dma((n_row * pieces,)),
            dma((n_row, pieces)),
            dma((n_row, pieces)),
            dma((samples, n_row)),
            dma((samples, n_row)),
        ],
        compiler_params=pltpu.CompilerParams(
            collective_id=0, has_side_effects=True, vmem_limit_bytes=60 * 1024 * 1024
        ),
    )(
        asym_id,
        valid_len,
        pair_repr,
        rel_embed,
        pair_gain.reshape(1, channels),
        bias_weight,
        tokens,
        token_gain,
        qkv_weight,
        out_weight,
    )


def solution(mesh):
    axes = tuple(mesh.shape[name] for name in ("job", "row", "col", "samp"))
    return jax.shard_map(
        functools.partial(per_device, axes),
        mesh=mesh,
        in_specs=(
            P(("job", "row"), ("col", "samp"), None),
            P("job"),
            P("job"),
            P(),
            P(),
            P(),
            P(("job", "col", "samp"), "row", None),
            P(),
            P(None, None, None, "row"),
            P(None, "row", None),
        ),
        out_specs=P(("job", "col", "samp"), "row", None),
        check_vma=False,
    )
```

time: 81.1 us -> 49.1 us (0.61)
  blocking collectives: 44.5 us -> 0 us
  Pallas kernels: 0 us -> 42.9 us
  between operations: 13.6 us -> 0.66 us
  starting transfers between devices: 6.35 us -> 0 us
  matrix products: 6.03 us -> 0 us
  other arithmetic: 5.46 us -> 0 us
  local copies, waits for them, and re-layouts: 3.84 us -> 5.37 us
    pallas_call x0 -> x1, Pallas kernels: none -> 42.9 us  [per_device(): pl.pallas_call(functools.partial(kernel, axes), out_shape=jax.ShapeDtypeS...]
    all_gather x2 -> x0, blocking collectives: 29.8 us -> none  [the longest x1 24 us: per_device(): lax.all_gather(normed, 'row', axis=1, tiled=True)]
    all_to_all x1 -> x0, blocking collectives: 14.7 us -> none  [per_device(): lax.all_to_all(head_out, 'row', split_axis=1, concat_axis=2, tiled=True)]
    all_to_all x1 -> x0, starting transfers between devices: 6.35 us -> none  [per_device(): lax.all_to_all(bias_tile, 'row', split_axis=0, concat_axis=1, tiled=True)]
    dot_general x12 -> x0, matrix products: 6.03 us -> none  [the longest x1 2.28 us: per_device(): jnp.dot(flattened, lax.all_gather(out_weight[0], 'row', axis=0, tiled=Tru...]
    unnamed x14 -> x3, local copies, waits for them, and re-layouts: 0.96 us -> 5.37 us
    lt x4 -> x0, other arithmetic: 2.61 us -> none  [per_device(): keymask = jnp.arange(total_tokens, dtype=jnp.int32) < valid_len[0]]
    convert_element_type x2 -> x0, other arithmetic: 1.14 us -> none  [the longest x1 0.99 us: bias_tile_of(): pair_repr.reshape(-1, channels).astype(jnp.float32)]
  transfers between devices with their start and end apart: 2 -> 0, of which waited for: 0 -> 0; matrix products, arithmetic and copies ran while one was open for 11% -> 0% of each run, Pallas kernels for 0% -> 0%
where the time goes in v1:
time: 49.1 us; the launch traced here: 48.9 us
  Pallas kernels  42.9 us (87%)
  local copies, waits for them, and re-layouts  5.37 us (11%)
  between operations  0.66 us (1%)
    pallas_call x1, Pallas kernels, per_device(): pl.pallas_call(functools.partial(kernel, axes), out_shape=jax.ShapeDtypeS...  42.9 us
    unnamed x3, local copies, waits for them, and re-layouts  5.37 us

profile of v1, /device:TPU:0, one launch (start us, length us, event | category | flops | bytes accessed | tf_op | source)
XLA Modules:
  0.0 48.9 jit_solution(7749173241073071037)
XLA Ops:
  0.7 1.4 %copy.11.bias_weight_hbm = bf16[128,16]{1,0:T(8,128)(2,1)} copy(bf16[128,16]{0,1:T(8,128)(2,1)} %param.15) | data formatting | bytes 8192 | tf_op args[5]
  2.1 2.3 %copy.12.qkv_hbm = bf16[1,3,768,192]{3,2,1,0:T(8,128)(2,1)} copy(bf16[1,3,768,192]{2,3,1,0:T(8,128)(2,1)} %param.18) | data formatting | bytes 1769472 | tf_op args[8]
  4.4 42.9 %shard_map.100 = bf16[4,32,768]{2,1,0:T(8,128)(2,1)} custom-call(s32[128]{0:T(128)} %asym.1, s32[1]{0:T(128)S(6)} %copy.14.valid, bf16[32,32,128]{2,1,0:T(8,128)(2,1)} %pair_hbm.1, bf16[128,128]{1,0:T(8,128)(2,1)} %rel_hbm.1, f32[1,128]{1,0:T(1,128)} %bitcast.1, bf16[128,16]{1,0:T(8,128)(2,1)} %copy.11.bias_weight_hbm, bf16[4,32,768]{2,1,0:T(8,128)(2,1)} %tokens_hbm.1, ...), custom_call_target="tpu_custom_call" | custom-call | tf_op jit(solution)/shard_map/pallas_call | solution.py:509
  47.3 1.6 %copy.15 = bf16[4,32,768]{2,1,0:T(8,128)(2,1)} copy(bf16[4,32,768]{2,1,0:T(8,128)(2,1)} %shard_map.100) | data formatting | bytes 393216

commit v2 on v1

--- a/solution.py
+++ b/solution.py
@@ -23,8 +23,9 @@
 
 def kernel(
     axes,
-    asym,
-    valid,
+    split,
+    asym_hbm,
+    valid_hbm,
     pair_hbm,
     rel_hbm,
     pair_gain_hbm,
@@ -34,6 +35,8 @@
     qkv_hbm,
     out_weight_hbm,
     out,
+    asym,
+    valid,
     pair,
     rel,
     pair_gain,
@@ -75,16 +78,19 @@
     bins = rel.shape[0]
     n_plane = n_col * n_samp
     plane = col * n_samp + samp
-    all_heads = bias_weight.shape[1]
+    all_heads = bias_weight.shape[0]
     local_heads = all_heads // n_row
     head_rows = bias_recv.shape[2]
     fold = LANES // tile_cols
     stripes = tile_rows // fold
     out_rows = ow.shape[1]
-    pieces = oz_recv.shape[0] // n_row
-    piece_rows = out_rows // pieces
+    row_pieces, col_pieces = split
+    pieces = row_pieces * col_pieces
+    piece_rows, piece_cols = out_rows // row_pieces, width // col_pieces
     shared = pieces > 1
-    group = job * n_samp + samp if shared else 0
+    group = (job * n_samp + samp if row_pieces > 1 else 0) * col_pieces + (
+        col if col_pieces > 1 else 0
+    )
     local_width = local_heads * HEAD_DIM
 
     def row_peer(k):
@@ -96,11 +102,18 @@
 
     def group_peer(k):
         other = lax.rem(group + k, pieces)
-        return {"job": lax.div(other, n_samp), "samp": lax.rem(other, n_samp)}, other
+        device, held = {}, lax.div(other, col_pieces)
+        if row_pieces > 1:
+            device.update(job=lax.div(held, n_samp), samp=lax.rem(held, n_samp))
+        if col_pieces > 1:
+            device.update(col=lax.rem(other, col_pieces))
+        return device, other
 
     loads = {}
     for index, (name, source, target) in enumerate(
         (
+            ("asym", asym_hbm, asym),
+            ("valid", valid_hbm, valid),
             ("pair", pair_hbm, pair),
             ("rel", rel_hbm, rel),
             ("pair_gain", pair_gain_hbm, pair_gain),
@@ -115,7 +128,7 @@
         pltpu.make_async_copy(tokens_hbm.at[s], tok.at[s, me], tok_local.at[s]) for s in range(samples)
     ]
     tok_loads[0].start()
-    for name in ("pair", "rel", "pair_gain", "bias_weight"):
+    for name in ("asym", "pair", "rel", "pair_gain", "bias_weight", "valid"):
         loads[name].start()
     for s in range(1, samples):
         tok_loads[s].start()
@@ -156,26 +169,24 @@
         def _():
             tok_copy(s, me, 1).start()
 
-    def pass_on(s):
-        for k in range(1, n_row):
-
-            @pl.when(me - k >= 0)
+    def pass_on(k, s):
+        @pl.when(me - k >= 0)
+        def _():
+            source = jnp.maximum(me - k, 0)
+            tok_copy(s, source, 0).wait_recv()
+
+            @pl.when(has_right)
             def _():
-                source = jnp.maximum(me - k, 0)
-                tok_copy(s, source, 0).wait_recv()
-
-                @pl.when(has_right)
-                def _():
-                    tok_copy(s, source, 0).start()
-
-            @pl.when(me + k < n_row)
+                tok_copy(s, source, 0).start()
+
+        @pl.when(me + k < n_row)
+        def _():
+            source = jnp.minimum(me + k, n_row - 1)
+            tok_copy(s, source, 1).wait_recv()
+
+            @pl.when(has_left)
             def _():
-                source = jnp.minimum(me + k, n_row - 1)
-                tok_copy(s, source, 1).wait_recv()
-
-                @pl.when(has_left)
-                def _():
-                    tok_copy(s, source, 1).start()
+                tok_copy(s, source, 1).start()
 
     def finish_tok_sends(s):
         for k in range(0, n_row):
@@ -188,10 +199,10 @@
             def _():
                 tok_copy(s, jnp.minimum(me + k, n_row - 1), 1).wait_send()
 
-    for s in range(min(2, samples)):
+    for s in range(samples):
         send_own(s)
 
-    for name in ("pair", "rel", "pair_gain", "bias_weight"):
+    for name in ("asym", "pair", "rel", "pair_gain", "bias_weight", "valid"):
         loads[name].wait()
     first_row, first_col = me * tile_rows, plane * tile_cols
     sub = lax.broadcasted_iota(jnp.int32, (tile_cols, LANES), 0)
@@ -200,7 +211,7 @@
     for j in range(tile_cols):
         col_chain = jnp.where(sub == j, asym[first_col + j], col_chain)
     reach = bins // 2 - 1
-    turned_weight = bias_weight[...].astype(jnp.float32).T.astype(jnp.bfloat16)
+    turned_weight = bias_weight[...]
     for t in range(stripes):
         hots, rows = [], []
         for q in range(fold):
@@ -277,7 +288,9 @@
     def ow_part(source, piece):
         if not shared:
             return ow.at[source]
-        return ow.at[source, pl.ds(pl.multiple_of(piece * piece_rows, piece_rows), piece_rows)]
+        first = pl.multiple_of(lax.div(piece, col_pieces) * piece_rows, piece_rows)
+        start = pl.multiple_of(lax.rem(piece, col_pieces) * piece_cols, piece_cols)
+        return ow.at[source, pl.ds(first, piece_rows), pl.ds(start, piece_cols)]
 
     def ow_row_copy(k):
         return pltpu.make_async_remote_copy(
@@ -333,9 +346,10 @@
     def project(s):
         rows = tok[s].reshape(total, width).astype(jnp.float32)
         normed = normalize(rows, token_gain[...]).astype(jnp.bfloat16)
-        query[s] = jnp.dot(normed, qkv[0], preferred_element_type=jnp.float32).astype(jnp.bfloat16)
-        key[s] = jnp.dot(normed, qkv[1], preferred_element_type=jnp.float32).astype(jnp.bfloat16)
-        value[s] = jnp.dot(normed, qkv[2], preferred_element_type=jnp.float32).astype(jnp.bfloat16)
+        for index, target in enumerate((query, key, value)):
+            target[s] = lax.dot_general(
+                normed, qkv[index], (((1,), (1,)), ((), ())), preferred_element_type=jnp.float32
+            ).astype(jnp.bfloat16)
 
     def attend(s):
         keys, values = key[s].astype(jnp.float32), value[s].astype(jnp.float32)
@@ -386,60 +400,58 @@
             att_copy(s, k).start()
         heads_in[me, s] = attended[s, me]
 
-    pass_on(0)
-    for s in range(2, min(3, samples)):
-        send_own(s)
+    loads["ow"].wait()
+    for k in range(1, n_row):
+        ow_row_copy(k).start()
+    for s in range(samples):
+        pass_on(1, s)
     for k in range(1, n_row):
         bias_row_wait(k)
         for m in range(1, n_plane):
             bias_plane_copy(k, m).start()
+    if shared:
+        for k in range(1, n_row):
+            ow_row_wait(k)
+            for m in range(1, pieces):
+                ow_group_copy(k, m).start()
+    for k in range(2, n_row - 1):
+        for s in range(samples):
+            pass_on(k, s)
     for name in ("token_gain", "qkv"):
         loads[name].wait()
-    project(0)
-    for s in range(1, samples):
-        pass_on(s)
-        if s + 2 < samples:
-            send_own(s + 2)
-        if s == 1:
-            loads["ow"].wait()
-            for k in range(1, n_row):
-                ow_row_copy(k).start()
+
+    own_bias.wait()
+    for k in range(n_row):
+        for m in range(1, n_plane):
+            bias_plane_wait(k, m)
+    lanes_at = lax.broadcasted_iota(jnp.int32, (head_rows, LANES), 1)
+    for tile in range(total // LANES):
+        padded = lanes_at[:stripes] + tile * LANES >= valid[0]
+        for r in range(n_row):
+            parts = [bias_recv[r, tile * fold + m] for m in range(fold)]
+            for q in range(fold):
+                whole = None
+                for m in range(fold):
+                    shift = ((m - q) % fold) * tile_cols
+                    turned = pltpu.roll(parts[m], shift, 1) if shift else parts[m]
+                    whole = (
+                        turned
+                        if whole is None
+                        else jnp.where(lanes_at >= m * tile_cols, turned, whole)
+                    )
+                at = r * tile_rows + q * stripes
+                for h in range(local_heads):
+                    bias[
+                        at : at + stripes,
+                        h * total + tile * LANES : h * total + (tile + 1) * LANES,
+                    ] = jnp.where(padded, -1e30, whole[h * stripes : (h + 1) * stripes])
+
+    for s in range(samples):
+        if n_row > 2:
+            pass_on(n_row - 1, s)
         project(s)
-        if s == 1:
-            own_bias.wait()
-            for k in range(n_row):
-                for m in range(1, n_plane):
-                    bias_plane_wait(k, m)
-            lanes_at = lax.broadcasted_iota(jnp.int32, (head_rows, LANES), 1)
-            for tile in range(total // LANES):
-                padded = lanes_at[:stripes] + tile * LANES >= valid[0]
-                for r in range(n_row):
-                    parts = [bias_recv[r, tile * fold + m] for m in range(fold)]
-                    for q in range(fold):
-                        whole = None
-                        for m in range(fold):
-                            shift = ((m - q) % fold) * tile_cols
-                            turned = pltpu.roll(parts[m], shift, 1) if shift else parts[m]
-                            whole = (
-                                turned
-                                if whole is None
-                                else jnp.where(lanes_at >= m * tile_cols, turned, whole)
-                            )
-                        at = r * tile_rows + q * stripes
-                        for h in range(local_heads):
-                            bias[
-                                at : at + stripes,
-                                h * total + tile * LANES : h * total + (tile + 1) * LANES,
-                            ] = jnp.where(padded, -1e30, whole[h * stripes : (h + 1) * stripes])
-        if s == 2 and shared:
-            for k in range(1, n_row):
-                ow_row_wait(k)
-                for m in range(1, pieces):
-                    ow_group_copy(k, m).start()
-        attend(s - 1)
-        give(s - 1)
-    attend(samples - 1)
-    give(samples - 1)
+        attend(s)
+        give(s)
 
     for k in range(1, n_row):
         if shared:
@@ -497,27 +509,28 @@
     tile_rows, tile_cols, channels = pair_repr.shape
     local_width = qkv_weight.shape[-1]
     out_rows = out_weight.shape[1]
-    pieces = n_job * n_samp
-    if out_rows % (16 * pieces) or pieces == 1:
-        pieces = 1
+    row_pieces = 1 if out_rows % (16 * n_job * n_samp) else n_job * n_samp
+    col_pieces = 1 if width % (LANES * n_col) else n_col
+    pieces = row_pieces * col_pieces
     stripes = tile_rows // (LANES // tile_cols)
     head_rows = local_heads * stripes
     bf16, f32 = jnp.bfloat16, jnp.float32
     dma = pltpu.SemaphoreType.DMA
     any_spec = pl.BlockSpec(memory_space=pl.ANY)
-    smem_spec = pl.BlockSpec(memory_space=pltpu.SMEM)
     return pl.pallas_call(
-        functools.partial(kernel, axes),
+        functools.partial(kernel, axes, (row_pieces, col_pieces)),
         out_shape=jax.ShapeDtypeStruct(tokens.shape, tokens.dtype),
-        in_specs=[smem_spec] * 2 + [any_spec] * 8,
+        in_specs=[any_spec] * 10,
         out_specs=pl.BlockSpec(memory_space=pltpu.VMEM),
         scratch_shapes=[
+            pltpu.SMEM(asym_id.shape, jnp.int32),
+            pltpu.SMEM(valid_len.shape, jnp.int32),
             pltpu.VMEM(pair_repr.shape, bf16),
             pltpu.VMEM(rel_embed.shape, bf16),
             pltpu.VMEM((1, channels), f32),
-            pltpu.VMEM(bias_weight.shape, bf16),
+            pltpu.VMEM(bias_weight.shape[::-1], bf16),
             pltpu.VMEM(token_gain.shape, f32),
-            pltpu.VMEM(qkv_weight.shape[1:], bf16),
+            pltpu.VMEM((3, local_width, width), bf16),
             pltpu.VMEM((samples, n_row, token_rows, width), bf16),
             pltpu.VMEM((n_row, out_rows, width), bf16),
             pltpu.VMEM((heads * stripes, LANES), f32),
@@ -528,7 +541,7 @@
             pltpu.VMEM((samples, total, local_width), bf16),
             pltpu.VMEM((samples, n_row, token_rows, local_width), bf16),
             pltpu.VMEM((n_row, samples, token_rows, local_width), bf16),
-            dma((7,)),
+            dma((9,)),
             dma((samples,)),
             dma((2, samples, n_row)),
             dma((samples, n_row)),
@@ -538,7 +551,7 @@
             dma((n_row, n_plane)),
             dma,
             dma((n_row,)),
-            dma((n_row * pieces,)),
+            dma((n_row,)),
             dma((n_row, pieces)),
             dma((n_row, pieces)),
             dma((samples, n_row)),
@@ -553,10 +566,10 @@
         pair_repr,
         rel_embed,
         pair_gain.reshape(1, channels),
-        bias_weight,
+        bias_weight.T,
         tokens,
         token_gain,
-        qkv_weight,
+        jnp.swapaxes(qkv_weight, 2, 3),
         out_weight,
     )
 

time: 49.1 us -> 34.3 us (0.70)
  Pallas kernels: 42.9 us -> 31.8 us
  local copies, waits for them, and re-layouts: 5.37 us -> 1.62 us
    pallas_call x1, Pallas kernels: 42.9 us -> 31.8 us  [per_device(): pl.pallas_call(functools.partial(kernel, axes, (row_pieces, col_pieces)),...]
    unnamed x3 -> x1, local copies, waits for them, and re-layouts: 5.37 us -> 1.62 us
where the time goes in v2:
time: 34.3 us; the launch traced here: 34.1 us
  Pallas kernels  31.8 us (93%)
  local copies, waits for them, and re-layouts  1.62 us (5%)
  between operations  0.66 us (2%)
    pallas_call x1, Pallas kernels, per_device(): pl.pallas_call(functools.partial(kernel, axes, (row_pieces, col_pieces)),...  31.8 us
    unnamed x1, local copies, waits for them, and re-layouts  1.62 us

profile of v2, /device:TPU:0, one launch (start us, length us, event | category | flops | bytes accessed | tf_op | source)
XLA Modules:
  0.0 34.1 jit_solution(14289638977249891718)
XLA Ops:
  0.7 31.8 %shard_map.100 = bf16[4,32,768]{2,1,0:T(8,128)(2,1)} custom-call(s32[128]{0:T(128)} %asym_hbm.1, s32[1]{0:T(128)S(6)} %copy.12.valid_hbm, bf16[32,32,128]{2,1,0:T(8,128)(2,1)} %pair_hbm.1, bf16[128,128]{1,0:T(8,128)(2,1)} %rel_hbm.1, f32[1,128]{1,0:T(1,128)} %bitcast.5, bf16[16,128]{1,0:T(8,128)(2,1)} %bitcast.4, bf16[4,32,768]{2,1,0:T(8,128)(2,1)} %tokens_hbm.1, ...), custom_call_target="tpu_custom_call" | custom-call | tf_op jit(solution)/shard_map/pallas_call | solution.py:520
  32.5 1.6 %copy.13 = bf16[4,32,768]{2,1,0:T(8,128)(2,1)} copy(bf16[4,32,768]{2,1,0:T(8,128)(2,1)} %shard_map.100) | data formatting | bytes 393216
